TPU v7x, 32 devices: a whole 2x2x4 slice. The times are simulated.
32 devices in a mesh: vocab: 16 (over z, y, x), pipe: 2 (over core).
Axes of the slice: x: 2, y: 2, z: 4, core: 2. Of those that a mesh axis runs over, the one named last changes fastest.
Arguments:
- hidden_a: bfloat16 [512, 4096], P('pipe', 'vocab'), parts along dimension 0, may hold values from -8 to 8, as said below
- labels_a: int32 [512], P('pipe'), parts along dimension 0, may hold values from 0 to 8191
- hidden_b: bfloat16 [512, 4096], P('pipe', 'vocab'), parts along dimension 0, may hold values from -8 to 8, as said below
- labels_b: int32 [512], P('pipe'), parts along dimension 0, may hold values from 0 to 8191
- loss_cotangent: float32 [512], P('pipe'), parts along dimension 0, may hold values from -192 to 192
- out_weight: bfloat16 [8192, 8192], P('pipe', 'vocab'), parts along dimension 0, may hold values from -0.28125 to 0.28125, as said below
Outputs:
- logits_a: bfloat16 [512, 8192], P('pipe', 'vocab'), parts along dimension 0
- loss_a: float32 [512], P('pipe'), parts along dimension 0
- amax_scale: float32 [2], P('pipe'), parts along dimension 0
- grad_hidden_b: bfloat16 [512, 4096], P('pipe', 'vocab'), parts along dimension 0
There are 2 independent parts, one for each index of `pipe`. A program takes and returns all parts, laid end to end along the dimension named above; each array names one. Nothing has to cross between parts.
Inputs may be any that keep to these rules, and one draw needn't show every extreme that they name: `hidden_a`: hidden states of order one. `hidden_b`: hidden states of order one. `out_weight`: entries of scale 3 over the square root of 4096.
All inputs are finite; a program needn't handle non-finite values. Where the computation divides by a largest or mean magnitude, that divisor is 1e-20 or more.
Results may differ from a plain program's by a relative error of at most 0.0048.
Values may be sent and summed in bfloat16 or wider, within the bound.
A program may use at most 64 MiB of HBM per device.

v0:
```python
import jax
import jax.numpy as jnp
from jax import lax
from jax.sharding import PartitionSpec as P


def shards(hidden_a, labels_a, hidden_b, labels_b, loss_cotangent, out_weight):
    vocab_rows = out_weight.shape[1]
    offset = lax.axis_index("vocab") * vocab_rows

    def accumulate(portion):
        return jnp.dot(portion, out_weight, preferred_element_type=jnp.float32)

    scores_a = accumulate(lax.all_gather(hidden_a, "vocab", axis=1, tiled=True))
    scores_b = accumulate(lax.all_gather(hidden_b, "vocab", axis=1, tiled=True))
    columns_a = offset + lax.broadcasted_iota(jnp.int32, scores_a.shape, 1)
    columns_b = offset + lax.broadcasted_iota(jnp.int32, scores_b.shape, 1)
    label_local = jnp.sum(jnp.where(columns_a == labels_a[:, None], scores_a, 0.0), axis=1)
    row_peak_a = jnp.max(scores_a, axis=1)
    abs_peak = jnp.max(jnp.abs(scores_a)).reshape(1)
    row_peak_b = jnp.max(scores_b, axis=1)
    peak_a, largest = lax.pmax((row_peak_a, abs_peak), "vocab")
    own_total_a = jnp.sum(jnp.exp(scores_a - peak_a[:, None]), axis=1)
    total_a, label_a = lax.psum((own_total_a, label_local), "vocab")
    peak_b = lax.pmax(row_peak_b, "vocab")
    own_total_b = jnp.sum(jnp.exp(scores_b - peak_b[:, None]), axis=1)
    total_b = lax.psum(own_total_b, "vocab")
    loss_a = jnp.log(total_a) + peak_a - label_a
    amax_scale = 448.0 / largest
    onehot = (columns_b == labels_b[:, None]).astype(jnp.float32)
    probs = jnp.exp(scores_b - peak_b[:, None]) / total_b[:, None]
    dlogits_b = ((probs - onehot) * loss_cotangent[:, None]).astype(jnp.bfloat16)
    grad_terms = lax.dot_general(
        dlogits_b, out_weight, (((1,), (1,)), ((), ())), preferred_element_type=jnp.float32
    )
    grad_hidden_b = lax.psum_scatter(grad_terms, "vocab", scatter_dimension=1, tiled=True).astype(
        jnp.bfloat16
    )
    return (scores_a.astype(jnp.bfloat16), loss_a, amax_scale, grad_hidden_b)


def solution(mesh):
    return jax.shard_map(
        shards,
        mesh=mesh,
        in_specs=(
            P("pipe", "vocab"),
            P("pipe"),
            P("pipe", "vocab"),
            P("pipe"),
            P("pipe"),
            P("pipe", "vocab"),
        ),
        out_specs=(P("pipe", "vocab"), P("pipe"), P("pipe"), P("pipe", "vocab")),
        check_vma=False,
    )
```

profile of v0, /device:TPU:0, one launch (start us, length us, event | category | flops | bytes accessed | tf_op | source)
XLA Modules:
  0.0 332.6 jit_solution(5259473569760511634)
XLA Ops:
  7.2 0.0 copy-start.2
  7.2 0.0 all-gather.3.cloned.1.call-start
  7.2 0.7 all-gather.3.cloned.1.call-update
  7.9 0.0 all-gather.5.cloned.1.call-start
  8.0 0.7 all-gather.5.cloned.1.call-update
  8.7 0.0 reduce-scatter.2.cloned.1.call-start
  8.7 69.5 %all-gather.3.cloned.1.call-done = bf16[256,4096]{1,0:T(8,128)(2,1)} async-done(((bf16[256,256]{1,0:T(8,128)(2,1)}), bf16[256,4096]{1,0:T(8,128)(2,1)}) %all-gather.3.cloned.1.call-update) | async-done | bytes 2097168 | tf_op jit(solution)/shard_map/all_gather | solution.py:14
  78.2 4.1 %fusion.7 = (f32[256]{0:T(256)S(1)}, f32[256,512]{1,0:T(8,128)S(1)}) fusion(bf16[256,4096]{1,0:T(8,128)(2,1)} %all-gather.3.cloned.1.call-done, bf16[4096,512]{1,0:T(8,128)(2,1)} %param.11), kind=kOutput, calls=%fused_computation.14 | convolution fusion | flops 1073872640 | bytes 6816768 | tf_op jit(solution)/shard_map/dot_general | solution.py:12
  82.3 38.8 %pmax.21 = f32[256]{0:T(256)S(1)} all-reduce(f32[256]{0:T(256)S(1)} %get-tuple-element.13), channel_id=1, replica_groups=mesh['vocab'=16,'pipe'=2] {'vocab'}, use_global_device_ids=true, to_apply=%region_1.2 | all-reduce | flops 256 | bytes 2048 | tf_op jit(solution)/shard_map/pmax | solution.py:22
  121.1 0.0 copy-done.2
  121.1 1.5 abs_reduce_fusion
  122.7 0.0 copy-start
  122.7 0.0 copy-start.1
  122.7 21.5 %all-gather.5.cloned.1.call-done = bf16[256,4096]{1,0:T(8,128)(2,1)} async-done(((bf16[256,256]{1,0:T(8,128)(2,1)}), bf16[256,4096]{1,0:T(8,128)(2,1)}) %all-gather.5.cloned.1.call-update) | async-done | bytes 2097168 | tf_op jit(solution)/shard_map/all_gather | solution.py:15
  144.2 4.1 %fusion.8 = (f32[256]{0:T(256)S(1)}, f32[256,512]{1,0:T(8,128)S(1)}) fusion(bf16[256,4096]{1,0:T(8,128)(2,1)} %all-gather.5.cloned.1.call-done, bf16[4096,512]{1,0:T(8,128)(2,1)} %param.11), kind=kOutput, calls=%fused_computation.15 | convolution fusion | flops 1073872640 | bytes 6816768 | tf_op jit(solution)/shard_map/dot_general | solution.py:12
  148.3 39.4 %all-reduce.1 = (f32[256]{0:T(256)S(1)}, f32[1]{0:T(128)}) all-reduce(f32[256]{0:T(256)S(1)} %get-tuple-element.15, f32[1]{0:T(128)} %bitcast), channel_id=1, replica_groups=mesh['vocab'=16,'pipe'=2] {'vocab'}, use_global_device_ids=true, to_apply=%region_9.10 | all-reduce | flops 257 | bytes 2056 | tf_op jit(solution)/shard_map/pmax | solution.py:25
  187.8 0.2 fusion
  188.0 36.6 %all-reduce = (f32[256]{0:T(256)S(1)}, f32[256]{0:T(256)S(1)}, f32[256]{0:T(256)S(1)}) all-reduce(f32[256]{0:T(256)S(1)} %get-tuple-element.5, f32[256]{0:T(256)S(1)} %get-tuple-element.6, f32[256]{0:T(256)S(1)} %fusion), channel_id=1, replica_groups=mesh['vocab'=16,'pipe'=2] {'vocab'}, use_global_device_ids=true, to_apply=%region_5.6 | all-reduce | flops 768 | bytes 6144 | tf_op jit(solution)/shard_map/psum | solution.py:24
  224.6 0.0 copy-done
  224.6 0.0 copy-done.1
  224.6 5.5 %fusion.1 = f32[256,4096]{1,0:T(8,128)} fusion(bf16[4096,512]{1,0:T(8,128)(2,1)} %param.11, f32[256,512]{1,0:T(8,128)S(1)} %get-tuple-element.16, f32[256]{0:T(256)S(1)} %copy-done, f32[256]{0:T(256)S(1)} %get-tuple-element.9, f32[256]{0:T(256)S(1)} %get-tuple-element.10, s32[512]{0:T(512)S(1)} %iota_add_fusion, s32[256]{0:T(256)S(1)} %copy-done.1), kind=kOutput, calls=%fused_computation.6 | convolution fusion | flops 1074659328 | bytes 8919040 | tf_op jit(solution)/shard_map/dot_general | solution.py:33
  230.1 0.0 reduce-scatter.2.cloned.1.call-update
  230.8 0.6 add_subtract_fusion
  231.3 91.9 %reduce-scatter.2.cloned.1.call-done = f32[256,256]{1,0:T(8,128)} async-done(((f32[256,4096]{1,0:T(8,128)}), f32[256,256]{1,0:T(8,128)}) %reduce-scatter.2.cloned.1.call-update) | async-done | bytes 262160 | tf_op jit(solution)/shard_map/reduce_scatter | solution.py:36
  323.3 1.6 convert_element_type.15
  (1 shorter events, 0.0 us)
Async XLA Ops:
  7.2 114.0 %copy-start.2 = (s32[256]{0:T(256)S(1)}, s32[256]{0:T(256)}, u32[]{:S(2)}) copy-start(s32[256]{0:T(256)} %param.7) | copy-start | bytes 3076
  7.2 71.0 %all-gather.3.cloned.1.call-start = ((), (), s32[]{:S(2)}) async-start(), calls=%async_computation.1 | async-start | bytes 2228224 | tf_op jit(solution)/shard_map/all_gather | solution.py:14
  7.9 136.3 %all-gather.5.cloned.1.call-start = ((), (), s32[]{:S(2)}) async-start(), calls=%async_computation.2 | async-start | bytes 2228224 | tf_op jit(solution)/shard_map/all_gather | solution.py:15
  8.7 314.6 %reduce-scatter.2.cloned.1.call-start = ((), (), s32[]{:S(2)}) async-start(), calls=%async_computation.3 | async-start | bytes 4456448 | tf_op jit(solution)/shard_map/reduce_scatter | solution.py:36
  122.7 101.9 %copy-start = (f32[256]{0:T(256)S(1)}, f32[256]{0:T(256)}, u32[]{:S(2)}) copy-start(f32[256]{0:T(256)} %param.10) | copy-start | bytes 3076
  122.7 101.9 %copy-start.1 = (s32[256]{0:T(256)S(1)}, s32[256]{0:T(256)}, u32[]{:S(2)}) copy-start(s32[256]{0:T(256)} %param.9) | copy-start | bytes 3076
Sparse Core Ops, SparseCore 0:
  10.7 67.4 all-gather.2
  80.9 63.2 all-gather.4
  230.2 93.0 reduce-scatter.1
where the time goes:
time: 333 us
  waiting for transfers between devices  184 us (55%)
  blocking collectives  115 us (35%)
  between operations  15.6 us (5%)
  matrix products  13.8 us (4%)
  other arithmetic  3.94 us (1%)
    reduce_scatter x1, waiting for transfers between devices, shards(): lax.psum_scatter(grad_terms, 'vocab', scatter_dimension=1, tiled=True)  91.9 us
    all_gather x1, waiting for transfers between devices, shards(): scores_a = accumulate(lax.all_gather(hidden_a, 'vocab', axis=1, tiled=True))  69.5 us
    pmax x1, blocking collectives, shards(): peak_b = lax.pmax(row_peak_b, 'vocab')  39.4 us
    pmax x1, blocking collectives, shards(): peak_a, largest = lax.pmax((row_peak_a, abs_peak), 'vocab')  38.8 us
    psum x1, blocking collectives, shards(): total_a, label_a = lax.psum((own_total_a, label_local), 'vocab')  36.6 us
    all_gather x1, waiting for transfers between devices, shards(): scores_b = accumulate(lax.all_gather(hidden_b, 'vocab', axis=1, tiled=True))  21.5 us
    dot_general x2, matrix products, accumulate(): return jnp.dot(portion, out_weight, preferred_element_type=jnp.float32)  8.29 us
  transfers between devices with their start and end apart: 3, of which 3 were waited for; matrix products, arithmetic and copies ran while one was open for 2% of the time, Pallas kernels for 0%

commit v1 on v0

--- a/solution.py
+++ b/solution.py
@@ -11,7 +11,11 @@
     def accumulate(portion):
         return jnp.dot(portion, out_weight, preferred_element_type=jnp.float32)
 
-    scores_a = accumulate(lax.all_gather(hidden_a, "vocab", axis=1, tiled=True))
+    scores_a = accumulate(
+        jnp.concatenate(
+            lax.all_to_all(jnp.stack([hidden_a] * lax.axis_size("vocab")), "vocab", 0, 0), axis=1
+        )
+    )
     scores_b = accumulate(lax.all_gather(hidden_b, "vocab", axis=1, tiled=True))
     columns_a = offset + lax.broadcasted_iota(jnp.int32, scores_a.shape, 1)
     columns_b = offset + lax.broadcasted_iota(jnp.int32, scores_b.shape, 1)

time: 333 us -> 305 us (0.916)
  waiting for transfers between devices: 184 us -> 135 us
  blocking collectives: 115 us -> 125 us
  starting transfers between devices: 0.11 us -> 8.42 us
    all_gather x1 -> x0, waiting for transfers between devices: 69.5 us -> none  [shards(): scores_a = accumulate(lax.all_gather(hidden_a, 'vocab', axis=1, tiled=True))]
    all_to_all x0 -> x1, waiting for transfers between devices: none -> 44.7 us  [shards(): lax.all_to_all(jnp.stack([hidden_a] * lax.axis_size('vocab')), 'vocab', 0...]
    all_gather x1, waiting for transfers between devices: 21.5 us -> 0.01 us  [shards(): scores_b = accumulate(lax.all_gather(hidden_b, 'vocab', axis=1, tiled=True))]
    pmax x1, blocking collectives: 38.8 us -> 49.4 us  [shards(): peak_a, largest = lax.pmax((row_peak_a, abs_peak), 'vocab')]
    all_to_all x0 -> x1, starting transfers between devices: none -> 8.34 us  [shards(): lax.all_to_all(jnp.stack([hidden_a] * lax.axis_size('vocab')), 'vocab', 0...]
  transfers between devices with their start and end apart: 3 -> 3, of which waited for: 3 -> 2; matrix products, arithmetic and copies ran while one was open for 2% -> 2% of each run, Pallas kernels for 0% -> 0%
where the time goes in v1:
time: 305 us; the launch traced here: 304 us
  waiting for transfers between devices  135 us (44%)
  blocking collectives  125 us (41%)
  between operations  15.9 us (5%)
  matrix products  13.2 us (4%)
  starting transfers between devices  8.42 us (3%)
  other arithmetic  3.95 us (1%)
    reduce_scatter x1, waiting for transfers between devices, shards(): lax.psum_scatter(grad_terms, 'vocab', scatter_dimension=1, tiled=True)  90 us
    pmax x1, blocking collectives, shards(): peak_a, largest = lax.pmax((row_peak_a, abs_peak), 'vocab')  49.4 us
    all_to_all x1, waiting for transfers between devices, shards(): lax.all_to_all(jnp.stack([hidden_a] * lax.axis_size('vocab')), 'vocab', 0...  44.7 us
    psum x1, blocking collectives, shards(): total_a, label_a = lax.psum((own_total_a, label_local), 'vocab')  38.6 us
    pmax x1, blocking collectives, shards(): peak_b = lax.pmax(row_peak_b, 'vocab')  37.2 us
    all_to_all x1, starting transfers between devices, shards(): lax.all_to_all(jnp.stack([hidden_a] * lax.axis_size('vocab')), 'vocab', 0...  8.34 us
    dot_general x2, matrix products, accumulate(): return jnp.dot(portion, out_weight, preferred_element_type=jnp.float32)  7.7 us
  transfers between devices with their start and end apart: 3, of which 2 were waited for; matrix products, arithmetic and copies ran while one was open for 2% of the time, Pallas kernels for 0%

profile of v1, /device:TPU:0, one launch (start us, length us, event | category | flops | bytes accessed | tf_op | source)
XLA Modules:
  0.0 304.5 jit_solution(11947473833509983023)
XLA Ops:
  7.2 1.0 copy.10
  8.2 1.5 stack.2
  9.7 8.3 %all-to-all-start = ((bf16[16,256,256]{1,2,0:T(8,128)(2,1)}), bf16[16,256,256]{1,2,0:T(8,128)(2,1)S(1)}, u32[]{:S(2)}, u32[]{:S(2)}) async-start(bf16[16,256,256]{1,2,0:T(8,128)(2,1)} %stack.2), calls=%async_computation | async-start | bytes 4194304 | tf_op jit(solution)/shard_map/all_to_all | solution.py:16
  18.0 0.0 all-gather.2.cloned.1.call-start
  18.1 0.7 all-gather.2.cloned.1.call-update
  18.8 0.0 reduce-scatter.2.cloned.1.call-start
  18.8 44.7 %all-to-all-done = bf16[16,256,256]{1,2,0:T(8,128)(2,1)S(1)} async-done(((bf16[16,256,256]{1,2,0:T(8,128)(2,1)}), bf16[16,256,256]{1,2,0:T(8,128)(2,1)S(1)}, u32[]{:S(2)}, u32[]{:S(2)}) %all-to-all-start) | async-done | bytes 2097184 | tf_op jit(solution)/shard_map/all_to_all | solution.py:16
  63.5 0.0 copy-start.2
  63.5 3.5 %fusion.7 = (f32[256]{0:T(256)S(1)}, f32[256,512]{1,0:T(8,128)S(1)}) fusion(bf16[256,4096]{0,1:T(8,128)(2,1)S(1)} %bitcast.9, bf16[4096,512]{1,0:T(8,128)(2,1)} %param.11), kind=kOutput, calls=%fused_computation.14 | convolution fusion | flops 1073872640 | bytes 6816768 | tf_op jit(solution)/shard_map/dot_general | solution.py:12
  67.1 49.4 %pmax.21 = f32[256]{0:T(256)S(1)} all-reduce(f32[256]{0:T(256)S(1)} %get-tuple-element.13), channel_id=1, replica_groups=mesh['vocab'=16,'pipe'=2] {'vocab'}, use_global_device_ids=true, to_apply=%region_1.2 | all-reduce | flops 256 | bytes 2048 | tf_op jit(solution)/shard_map/pmax | solution.py:26
  116.4 0.0 copy-done.2
  116.4 1.5 abs_reduce_fusion
  118.0 0.0 copy-start
  118.0 0.0 copy-start.1
  118.0 0.0 all-gather.2.cloned.1.call-done
  118.0 4.2 %fusion.8 = (f32[256]{0:T(256)S(1)}, f32[256,512]{1,0:T(8,128)S(1)}) fusion(bf16[256,4096]{1,0:T(8,128)(2,1)} %all-gather.2.cloned.1.call-done, bf16[4096,512]{1,0:T(8,128)(2,1)} %param.11), kind=kOutput, calls=%fused_computation.15 | convolution fusion | flops 1073872640 | bytes 6816768 | tf_op jit(solution)/shard_map/dot_general | solution.py:12
  122.1 37.2 %all-reduce.1 = (f32[256]{0:T(256)S(1)}, f32[1]{0:T(128)}) all-reduce(f32[256]{0:T(256)S(1)} %get-tuple-element.15, f32[1]{0:T(128)} %bitcast.2), channel_id=1, replica_groups=mesh['vocab'=16,'pipe'=2] {'vocab'}, use_global_device_ids=true, to_apply=%region_9.10 | all-reduce | flops 257 | bytes 2056 | tf_op jit(solution)/shard_map/pmax | solution.py:29
  159.3 0.2 fusion
  159.6 38.6 %all-reduce = (f32[256]{0:T(256)S(1)}, f32[256]{0:T(256)S(1)}, f32[256]{0:T(256)S(1)}) all-reduce(f32[256]{0:T(256)S(1)} %get-tuple-element.5, f32[256]{0:T(256)S(1)} %get-tuple-element.6, f32[256]{0:T(256)S(1)} %fusion), channel_id=1, replica_groups=mesh['vocab'=16,'pipe'=2] {'vocab'}, use_global_device_ids=true, to_apply=%region_5.6 | all-reduce | flops 768 | bytes 6144 | tf_op jit(solution)/shard_map/psum | solution.py:28
  198.1 0.0 copy-done
  198.1 0.0 copy-done.1
  198.1 5.5 %fusion.1 = f32[256,4096]{1,0:T(8,128)} fusion(bf16[4096,512]{1,0:T(8,128)(2,1)} %param.11, f32[256,512]{1,0:T(8,128)S(1)} %get-tuple-element.16, f32[256]{0:T(256)S(1)} %copy-done, f32[256]{0:T(256)S(1)} %get-tuple-element.9, f32[256]{0:T(256)S(1)} %get-tuple-element.10, s32[512]{0:T(512)S(1)} %iota_add_fusion, s32[256]{0:T(256)S(1)} %copy-done.1), kind=kOutput, calls=%fused_computation.6 | convolution fusion | flops 1074659328 | bytes 8919040 | tf_op jit(solution)/shard_map/dot_general | solution.py:37
  203.6 0.0 reduce-scatter.2.cloned.1.call-update
  204.3 0.6 add_subtract_fusion
  204.9 90.0 %reduce-scatter.2.cloned.1.call-done = f32[256,256]{1,0:T(8,128)} async-done(((f32[256,4096]{1,0:T(8,128)}), f32[256,256]{1,0:T(8,128)}) %reduce-scatter.2.cloned.1.call-update) | async-done | bytes 262160 | tf_op jit(solution)/shard_map/reduce_scatter | solution.py:40
  294.9 1.6 convert_element_type.15
  (1 shorter events, 0.0 us)
Async XLA Ops:
  9.7 53.9 %all-to-all-start = ((bf16[16,256,256]{1,2,0:T(8,128)(2,1)}), bf16[16,256,256]{1,2,0:T(8,128)(2,1)S(1)}, u32[]{:S(2)}, u32[]{:S(2)}) async-start(bf16[16,256,256]{1,2,0:T(8,128)(2,1)} %stack.2), calls=%async_computation | async-start | bytes 4194304 | tf_op jit(solution)/shard_map/all_to_all | solution.py:16
  18.0 100.0 %all-gather.2.cloned.1.call-start = ((), (), s32[]{:S(2)}) async-start(), calls=%async_computation.2 | async-start | bytes 2228224 | tf_op jit(solution)/shard_map/all_gather | solution.py:19
  18.8 276.1 %reduce-scatter.2.cloned.1.call-start = ((), (), s32[]{:S(2)}) async-start(), calls=%async_computation.3 | async-start | bytes 4456448 | tf_op jit(solution)/shard_map/reduce_scatter | solution.py:40
  63.5 52.9 %copy-start.2 = (s32[256]{0:T(256)S(1)}, s32[256]{0:T(256)}, u32[]{:S(2)}) copy-start(s32[256]{0:T(256)} %param.7) | copy-start | bytes 3076
  118.0 80.2 %copy-start = (f32[256]{0:T(256)S(1)}, f32[256]{0:T(256)}, u32[]{:S(2)}) copy-start(f32[256]{0:T(256)} %param.10) | copy-start | bytes 3076
  118.0 80.2 %copy-start.1 = (s32[256]{0:T(256)S(1)}, s32[256]{0:T(256)}, u32[]{:S(2)}) copy-start(s32[256]{0:T(256)} %param.9) | copy-start | bytes 3076
Sparse Core Ops, SparseCore 0:
  21.6 77.6 all-gather.1
  203.8 91.0 reduce-scatter.1

commit v2 on v0

--- a/solution.py
+++ b/solution.py
@@ -12,7 +12,7 @@
         return jnp.dot(portion, out_weight, preferred_element_type=jnp.float32)
 
     scores_a = accumulate(lax.all_gather(hidden_a, "vocab", axis=1, tiled=True))
-    scores_b = accumulate(lax.all_gather(hidden_b, "vocab", axis=1, tiled=True))
+    scores_b = accumulate(jnp.concatenate(lax.all_gather(hidden_b, "vocab"), axis=1))
     columns_a = offset + lax.broadcasted_iota(jnp.int32, scores_a.shape, 1)
     columns_b = offset + lax.broadcasted_iota(jnp.int32, scores_b.shape, 1)
     label_local = jnp.sum(jnp.where(columns_a == labels_a[:, None], scores_a, 0.0), axis=1)

time: 333 us -> 333 us (level)
  transfers between devices with their start and end apart: 3 -> 3, of which waited for: 3 -> 3; matrix products, arithmetic and copies ran while one was open for 2% -> 1% of each run, Pallas kernels for 0% -> 0%
where the time goes in v2:
time: 333 us
  waiting for transfers between devices  181 us (54%)
  blocking collectives  116 us (35%)
  between operations  15.6 us (5%)
  matrix products  13.2 us (4%)
  other arithmetic  3.94 us (1%)
    reduce_scatter x1, waiting for transfers between devices, shards(): lax.psum_scatter(grad_terms, 'vocab', scatter_dimension=1, tiled=True)  91.9 us
    all_gather x1, waiting for transfers between devices, shards(): scores_a = accumulate(lax.all_gather(hidden_a, 'vocab', axis=1, tiled=True))  69.5 us
    pmax x1, blocking collectives, shards(): peak_b = lax.pmax(row_peak_b, 'vocab')  40.2 us
    pmax x1, blocking collectives, shards(): peak_a, largest = lax.pmax((row_peak_a, abs_peak), 'vocab')  39 us
    psum x1, blocking collectives, shards(): total_a, label_a = lax.psum((own_total_a, label_local), 'vocab')  36.6 us
    all_gather x1, waiting for transfers between devices, shards(): lax.all_gather(hidden_b, 'vocab')  18.7 us
    dot_general x2, matrix products, accumulate(): return jnp.dot(portion, out_weight, preferred_element_type=jnp.float32)  7.68 us
  transfers between devices with their start and end apart: 3, of which 3 were waited for; matrix products, arithmetic and copies ran while one was open for 1% of the time, Pallas kernels for 0%

profile of v2, /device:TPU:0, one launch (start us, length us, event | category | flops | bytes accessed | tf_op | source)
XLA Modules:
  0.0 332.9 jit_solution(17524253193437653382)
XLA Ops:
  7.2 0.0 all-gather.4.cloned.1.call-start
  7.2 0.7 all-gather.4.cloned.1.call-update
  7.9 0.0 all-gather.6.cloned.1.call-start
  7.9 0.7 all-gather.6.cloned.1.call-update
  8.6 0.0 reduce-scatter.2.cloned.1.call-start
  8.7 69.5 %all-gather.4.cloned.1.call-done = bf16[256,4096]{1,0:T(8,128)(2,1)} async-done(((bf16[256,256]{1,0:T(8,128)(2,1)}), bf16[256,4096]{1,0:T(8,128)(2,1)}) %all-gather.4.cloned.1.call-update) | async-done | bytes 2097168 | tf_op jit(solution)/shard_map/all_gather | solution.py:14
  78.2 4.1 %fusion.7 = (f32[256]{0:T(256)S(1)}, f32[256,512]{1,0:T(8,128)S(1)}) fusion(bf16[256,4096]{1,0:T(8,128)(2,1)} %all-gather.4.cloned.1.call-done, bf16[4096,512]{1,0:T(8,128)(2,1)} %param.11), kind=kOutput, calls=%fused_computation.14 | convolution fusion | flops 1073872640 | bytes 6816768 | tf_op jit(solution)/shard_map/dot_general | solution.py:12
  82.3 39.0 %pmax.21 = f32[256]{0:T(256)S(1)} all-reduce(f32[256]{0:T(256)S(1)} %get-tuple-element.13), channel_id=1, replica_groups=mesh['vocab'=16,'pipe'=2] {'vocab'}, use_global_device_ids=true, to_apply=%region_1.2 | all-reduce | flops 256 | bytes 2048 | tf_op jit(solution)/shard_map/pmax | solution.py:22
  121.3 18.7 %all-gather.6.cloned.1.call-done = bf16[4096,256]{1,0:T(8,128)(2,1)} async-done(((bf16[256,256]{1,0:T(8,128)(2,1)}), bf16[4096,256]{1,0:T(8,128)(2,1)}) %all-gather.6.cloned.1.call-update) | async-done | bytes 2097168 | tf_op jit(solution)/shard_map/all_gather | solution.py:15
  140.0 2.8 copy.10
  142.8 0.0 copy-start.2
  142.9 0.0 copy-start
  142.9 0.0 copy-start.1
  142.9 3.5 %fusion.8 = (f32[256]{0:T(256)S(1)}, f32[256,512]{1,0:T(8,128)S(1)}) fusion(bf16[256,4096]{0,1:T(8,128)(2,1)S(1)} %bitcast.11, bf16[4096,512]{1,0:T(8,128)(2,1)} %param.11), kind=kOutput, calls=%fused_computation.15 | convolution fusion | flops 1073872640 | bytes 6816768 | tf_op jit(solution)/shard_map/dot_general | solution.py:12
  146.4 0.0 copy-done.2
  146.4 1.5 abs_reduce_fusion
  148.0 40.2 %all-reduce.1 = (f32[256]{0:T(256)S(1)}, f32[1]{0:T(128)}) all-reduce(f32[256]{0:T(256)S(1)} %get-tuple-element.15, f32[1]{0:T(128)} %bitcast), channel_id=1, replica_groups=mesh['vocab'=16,'pipe'=2] {'vocab'}, use_global_device_ids=true, to_apply=%region_9.10 | all-reduce | flops 257 | bytes 2056 | tf_op jit(solution)/shard_map/pmax | solution.py:25
  188.2 0.2 fusion
  188.4 36.6 %all-reduce = (f32[256]{0:T(256)S(1)}, f32[256]{0:T(256)S(1)}, f32[256]{0:T(256)S(1)}) all-reduce(f32[256]{0:T(256)S(1)} %get-tuple-element.5, f32[256]{0:T(256)S(1)} %get-tuple-element.6, f32[256]{0:T(256)S(1)} %fusion), channel_id=1, replica_groups=mesh['vocab'=16,'pipe'=2] {'vocab'}, use_global_device_ids=true, to_apply=%region_5.6 | all-reduce | flops 768 | bytes 6144 | tf_op jit(solution)/shard_map/psum | solution.py:24
  225.0 0.0 copy-done
  225.0 0.0 copy-done.1
  225.0 5.5 %fusion.1 = f32[256,4096]{1,0:T(8,128)} fusion(bf16[4096,512]{1,0:T(8,128)(2,1)} %param.11, f32[256,512]{1,0:T(8,128)S(1)} %get-tuple-element.16, f32[256]{0:T(256)S(1)} %copy-done, f32[256]{0:T(256)S(1)} %get-tuple-element.9, f32[256]{0:T(256)S(1)} %get-tuple-element.10, s32[512]{0:T(512)S(1)} %iota_add_fusion, s32[256]{0:T(256)S(1)} %copy-done.1), kind=kOutput, calls=%fused_computation.6 | convolution fusion | flops 1074659328 | bytes 8919040 | tf_op jit(solution)/shard_map/dot_general | solution.py:33
  230.4 0.0 reduce-scatter.2.cloned.1.call-update
  231.2 0.6 add_subtract_fusion
  231.7 91.9 %reduce-scatter.2.cloned.1.call-done = f32[256,256]{1,0:T(8,128)} async-done(((f32[256,4096]{1,0:T(8,128)}), f32[256,256]{1,0:T(8,128)}) %reduce-scatter.2.cloned.1.call-update) | async-done | bytes 262160 | tf_op jit(solution)/shard_map/reduce_scatter | solution.py:36
  323.6 1.6 convert_element_type.15
  (1 shorter events, 0.0 us)
Async XLA Ops:
  7.2 71.0 %all-gather.4.cloned.1.call-start = ((), (), s32[]{:S(2)}) async-start(), calls=%async_computation.1 | async-start | bytes 2228224 | tf_op jit(solution)/shard_map/all_gather | solution.py:14
  7.9 132.1 %all-gather.6.cloned.1.call-start = ((), (), s32[]{:S(2)}) async-start(), calls=%async_computation.3 | async-start | bytes 2228224 | tf_op jit(solution)/shard_map/all_gather | solution.py:15
  8.6 315.0 %reduce-scatter.2.cloned.1.call-start = ((), (), s32[]{:S(2)}) async-start(), calls=%async_computation.2 | async-start | bytes 4456448 | tf_op jit(solution)/shard_map/reduce_scatter | solution.py:36
  142.8 3.6 %copy-start.2 = (s32[256]{0:T(256)S(1)}, s32[256]{0:T(256)}, u32[]{:S(2)}) copy-start(s32[256]{0:T(256)} %param.7) | copy-start | bytes 3076
  142.9 82.1 %copy-start = (f32[256]{0:T(256)S(1)}, f32[256]{0:T(256)}, u32[]{:S(2)}) copy-start(f32[256]{0:T(256)} %param.10) | copy-start | bytes 3076
  142.9 82.1 %copy-start.1 = (s32[256]{0:T(256)S(1)}, s32[256]{0:T(256)}, u32[]{:S(2)}) copy-start(s32[256]{0:T(256)} %param.9) | copy-start | bytes 3076
Sparse Core Ops, SparseCore 0:
  10.7 67.4 all-gather.3
  80.9 58.9 all-gather.5
  230.6 93.0 reduce-scatter.1
